TPU v7x, 32 devices: a whole 2x2x4 slice. The times are simulated.
32 devices in a mesh: gx: 2 (over core), gy: 4 (over y, x), ma: 4 (over z).
Axes of the slice: x: 2, y: 2, z: 4, core: 2. Of those that a mesh axis runs over, the one named last changes fastest.
Arguments:
- object_field: float32 [2, 256, 1024], P(None, 'gx', 'gy'), may hold values from -5 to 5
- probe_modes: float32 [8, 2, 256, 256], P('ma'), may hold values from -1.5 to 1.5
- measured: float32 [2, 4, 2, 256, 256], P('gx', 'gy'), may hold values from 0.1 to 4
- positions: int32 [2, 4, 2, 2], P('gx', 'gy'), may hold values from 0 to 255, as said below
- slot_counts: int32 [2, 4], P('gx', 'gy'), may hold values from 1 to 2, as said below
Outputs:
- updated_object: float32 [2, 256, 1024], P(None, 'gx', 'gy')
Inputs may be any that keep to these rules, and one draw needn't show every extreme that they name: positions[a, b, s] holds a row 0 to 127 and a column 0 to 255 of tile (a, b); slots s >= slot_counts[a, b] are unused. `slot_counts`: some tile uses all 2 slots.
All inputs are finite; a program needn't handle non-finite values.
Results may differ from a plain program's by a relative error of at most 0.0023.
Values sent between devices are 32-bit elements; how exact they have to be, the bound alone decides.
A program may use at most 64 MiB of HBM per device.

v0:
```python
import math
import jax
import jax.numpy as jnp
from jax import lax
from jax.sharding import PartitionSpec as P

OUTER = 2
DAMPING = 1.0


def padded_2(block, sides, width):
    for axis, dim in sides:
        count = lax.axis_size(axis)
        forward = [(i, i + 1) for i in range(count - 1)]
        backward = [(target, source) for source, target in forward]
        low = lax.ppermute(
            lax.slice_in_dim(block, block.shape[dim] - width, None, axis=dim), axis, forward
        )
        high = lax.ppermute(lax.slice_in_dim(block, 0, width, axis=dim), axis, backward)
        block = jnp.concatenate([low, block, high], axis=dim)
    return block


def dft_tables(patch_width):
    ladder = jnp.arange(patch_width, dtype=jnp.int32)
    phases = ladder[:, None] * ladder[None, :] % patch_width
    angles = phases.astype(jnp.float32) * (2.0 * math.pi / patch_width)
    factor = 1.0 / math.sqrt(patch_width)
    real_part = jnp.cos(angles) * factor
    imag_part = -jnp.sin(angles) * factor
    table_one = jnp.concatenate(
        [jnp.concatenate([real_part, -imag_part], 1), jnp.concatenate([imag_part, real_part], 1)], 0
    ).astype(jnp.bfloat16)
    table_two = jnp.concatenate(
        [jnp.concatenate([real_part, imag_part], 1), jnp.concatenate([-imag_part, real_part], 1)], 0
    ).astype(jnp.bfloat16)
    return (table_one, table_two)


def forward_transform(wavefield, tables):
    patch_width = wavefield.shape[-1]
    halfway = jnp.einsum(
        "pqci,bcik->bpqk",
        tables[0].reshape(2, patch_width, 2, patch_width),
        wavefield,
        preferred_element_type=jnp.float32,
    ).astype(jnp.bfloat16)
    return jnp.einsum(
        "bcik,ckl->bil",
        halfway,
        tables[1].reshape(2, patch_width, 2 * patch_width),
        preferred_element_type=jnp.float32,
    )


def adjoint_transform(weighted, tables):
    patch_width = weighted.shape[1]
    halfway = jnp.einsum(
        "bik,kl->bil", weighted, tables[0], preferred_element_type=jnp.float32
    ).astype(jnp.bfloat16)
    return jnp.einsum(
        "pqci,bicl->bpql",
        tables[1].reshape(2, patch_width, 2, patch_width),
        halfway.reshape(halfway.shape[0], patch_width, 2, patch_width),
        preferred_element_type=jnp.float32,
    )


def exit_waves(probe_modes, windows):
    probe_real = probe_modes[None, :, 0]
    probe_imag = probe_modes[None, :, 1]
    window_real = windows[:, None, 0]
    window_imag = windows[:, None, 1]
    real_part = probe_real * window_real - probe_imag * window_imag
    imag_part = probe_real * window_imag + probe_imag * window_real
    wavefield = jnp.stack([real_part, imag_part], 2).astype(jnp.bfloat16)
    return wavefield.reshape(-1, 2, probe_modes.shape[-1], probe_modes.shape[-1])


def intensity_part(spectra, mode_count):
    patch_width = spectra.shape[1]
    grouped = spectra.reshape(-1, mode_count, patch_width, 2 * patch_width)
    squared = grouped * grouped
    return jnp.sum(squared[..., :patch_width] + squared[..., patch_width:], axis=1)


def change_part(spectra, moved_spectra, mode_count):
    patch_width = spectra.shape[1]
    grouped = spectra.reshape(-1, mode_count, patch_width, 2 * patch_width)
    shifted = moved_spectra.reshape(-1, mode_count, patch_width, 2 * patch_width)
    product = grouped * shifted
    return 2.0 * jnp.sum(product[..., :patch_width] + product[..., patch_width:], axis=1)


def mode_images(weights, spectra, probe_modes, tables):
    mode_count = probe_modes.shape[0]
    patch_width = probe_modes.shape[-1]
    doubled = jnp.concatenate([weights, weights], -1)
    grouped = spectra.reshape(-1, mode_count, patch_width, 2 * patch_width)
    weighted = (2.0 * grouped * doubled[:, None]).astype(jnp.bfloat16)
    returned = adjoint_transform(weighted.reshape(-1, patch_width, 2 * patch_width), tables)
    returned = returned.reshape(-1, mode_count, 2, patch_width, patch_width)
    probe_real = probe_modes[None, :, 0]
    probe_imag = probe_modes[None, :, 1]
    real_part = jnp.sum(probe_real * returned[:, :, 0] + probe_imag * returned[:, :, 1], axis=1)
    imag_part = jnp.sum(probe_real * returned[:, :, 1] - probe_imag * returned[:, :, 0], axis=1)
    return jnp.stack([real_part, imag_part], 1)


def fold_edges(widened, axis_dim, length, rim_width):
    middle = lax.slice_in_dim(widened, 2 * rim_width, 2 * rim_width + length, axis=axis_dim)
    low_rim = lax.slice_in_dim(widened, 0, rim_width, axis=axis_dim)
    high_rim = lax.slice_in_dim(
        widened, length + 3 * rim_width, length + 4 * rim_width, axis=axis_dim
    )
    low_pads = [(0, 0), (0, 0), (0, 0)]
    high_pads = [(0, 0), (0, 0), (0, 0)]
    low_pads[axis_dim] = (0, length - rim_width)
    high_pads[axis_dim] = (length - rim_width, 0)
    return middle + jnp.pad(low_rim, low_pads) + jnp.pad(high_rim, high_pads)


def shards(object_field, probe_modes, measured, positions, slot_counts):
    patch_width = probe_modes.shape[-1]
    mode_count = probe_modes.shape[0]
    rim_width = patch_width // 2
    tile_rows = object_field.shape[1]
    tile_cols = object_field.shape[2]
    slot_count = measured.shape[2]
    share_rows = tile_rows // lax.axis_size("ma")
    tables = dft_tables(patch_width)
    targets = measured[0, 0]
    centres = positions[0, 0]
    live_mask = (jnp.arange(slot_count, dtype=jnp.int32) < slot_counts[0, 0]).astype(jnp.float32)[
        :, None, None
    ]
    anchor = jnp.zeros((), jnp.int32)

    def spectra_of(current):
        padded = padded_2(current, (("gx", 1), ("gy", 2)), rim_width)
        windows = jnp.stack(
            [
                lax.dynamic_slice(
                    padded,
                    (anchor, centres[slot_index, 0], centres[slot_index, 1]),
                    (2, patch_width, patch_width),
                )
                for slot_index in range(slot_count)
            ],
            0,
        )
        return forward_transform(exit_waves(probe_modes, windows), tables)

    def mode_total(partial_value):
        return lax.psum(partial_value, "ma")

    def combine(folded):
        summed = lax.psum(folded, "ma")
        return summed

    def project(weights, spectra):
        pieces = mode_images(weights, spectra, probe_modes, tables)
        extended = jnp.zeros((2, tile_rows + patch_width, tile_cols + patch_width), jnp.float32)
        for slot_index in range(slot_count):
            corner = (anchor, centres[slot_index, 0], centres[slot_index, 1])
            extended = lax.dynamic_update_slice(
                extended,
                lax.dynamic_slice(extended, corner, (2, patch_width, patch_width))
                + pieces[slot_index],
                corner,
            )
        widened = padded_2(extended, (("gx", 1), ("gy", 2)), rim_width)
        folded = fold_edges(fold_edges(widened, 1, tile_rows, rim_width), 2, tile_cols, rim_width)
        result = combine(folded)
        return result

    def local_sum(first_vec, second_vec):
        first_vec = lax.dynamic_slice_in_dim(
            first_vec, lax.axis_index("ma") * share_rows, share_rows, 1
        )
        second_vec = lax.dynamic_slice_in_dim(
            second_vec, lax.axis_index("ma") * share_rows, share_rows, 1
        )
        return jnp.sum(first_vec * second_vec)

    current = object_field
    for outer_step in range(OUTER):
        spectra = spectra_of(current)
        misfit = live_mask * (mode_total(intensity_part(spectra, mode_count)) - targets)
        gradient = project(misfit, spectra)
        residual = -gradient
        direction = residual
        norm_now = lax.psum(local_sum(residual, residual), ("gx", "gy", "ma"))
        moved_spectra = spectra_of(direction)
        change = live_mask * mode_total(change_part(spectra, moved_spectra, mode_count))
        applied = project(change, spectra) + DAMPING * direction
        step_size = norm_now / lax.psum(local_sum(direction, applied), ("gx", "gy", "ma"))
        update = step_size * direction
        residual = residual - step_size * applied
        current = current + update
    return current


def solution(mesh):
    return jax.shard_map(
        shards,
        mesh=mesh,
        in_specs=(
            P(None, "gx", "gy"),
            P("ma", None, None, None),
            P("gx", "gy", None, None, None),
            P("gx", "gy", None, None),
            P("gx", "gy"),
        ),
        out_specs=P(None, "gx", "gy"),
        check_vma=False,
    )
```

profile of v0, /device:TPU:0, one launch (start us, length us, event | category | flops | bytes accessed | tf_op | source)
XLA Modules:
  0.0 797.4 jit_solution(15070351154825093424)
XLA Ops:
  45.2 36.4 %all-reduce.15.cloned.1.call-done = f32[2,256,256]{2,1,0:T(8,128)} async-done(((f32[2,256,256]{2,1,0:T(8,128)}), f32[2,256,256]{2,1,0:T(8,128)}) %all-reduce.15.cloned.1.call-update) | async-done | bytes 524304 | tf_op jit(solution)/shard_map/psum | solution.py:155
  117.4 12.9 %collective-permute-done.6 = f32[2,640,128]{1,2,0:T(8,128)S(1)} collective-permute-done((f32[2,640,128]{1,2,0:T(8,128)S(1)}, f32[2,640,128]{1,2,0:T(8,128)S(1)}, u32[]{:S(2)}, u32[]{:S(2)}) %collective-permute-start.6) | collective-permute-done | bytes 655392 | tf_op jit(solution)/shard_map/ppermute | solution.py:16
  130.4 16.7 %collective-permute-done.7 = f32[2,640,128]{1,2,0:T(8,128)S(1)} collective-permute-done((f32[2,640,128]{1,2,0:T(8,128)S(1)}, f32[2,640,128]{1,2,0:T(8,128)S(1)}, u32[]{:S(2)}, u32[]{:S(2)}) %collective-permute-start.7) | collective-permute-done | bytes 655392 | tf_op jit(solution)/shard_map/ppermute | solution.py:19
  148.6 33.7 %all-reduce.17.cloned.1.call-done = f32[2,128,256]{1,2,0:T(8,128)} async-done(((f32[2,128,256]{1,2,0:T(8,128)}), f32[2,128,256]{1,2,0:T(8,128)}) %all-reduce.17.cloned.1.call-update) | async-done | bytes 262160 | tf_op jit(solution)/shard_map/psum | solution.py:158
  200.2 10.3 %collective-permute-done.11 = f32[2,384,128]{1,2,0:T(8,128)S(1)} collective-permute-done((f32[2,384,128]{1,2,0:T(8,128)S(1)}, f32[2,384,128]{1,2,0:T(8,128)S(1)}, u32[]{:S(2)}, u32[]{:S(2)}) %collective-permute-start.11) | collective-permute-done | bytes 393248 | tf_op jit(solution)/shard_map/ppermute | solution.py:19
  218.3 37.7 %all-reduce.19.cloned.1.call-done = f32[2,256,256]{2,1,0:T(8,128)} async-done(((f32[2,256,256]{2,1,0:T(8,128)}), f32[2,256,256]{2,1,0:T(8,128)}) %all-reduce.19.cloned.1.call-update) | async-done | bytes 524304 | tf_op jit(solution)/shard_map/psum | solution.py:155
  273.6 8.2 %dynamic_update_slice.27 = f32[2,384,512]{1,2,0:T(8,128)S(1)} dynamic-update-slice(f32[2,384,512]{1,2,0:T(8,128)S(1)} %dynamic_update_slice.26, f32[2,256,256]{1,2,0:T(8,128)} %fusion.47, s32[]{:T(128)} %constant.15.clone.1, s32[]{:T(128)S(6)} %select_n.33, s32[]{:T(128)S(6)} %select_n.34) | dynamic-update-slice | bytes 1048580 | tf_op jit(solution)/shard_map/dynamic_update_slice | solution.py:166
  291.8 12.9 %collective-permute-done.14 = f32[2,640,128]{1,2,0:T(8,128)S(1)} collective-permute-done((f32[2,640,128]{1,2,0:T(8,128)S(1)}, f32[2,640,128]{1,2,0:T(8,128)S(1)}, u32[]{:S(2)}, u32[]{:S(2)}) %collective-permute-start.14) | collective-permute-done | bytes 655392 | tf_op jit(solution)/shard_map/ppermute | solution.py:16
  304.7 16.7 %collective-permute-done.15 = f32[2,640,128]{1,2,0:T(8,128)S(1)} collective-permute-done((f32[2,640,128]{1,2,0:T(8,128)S(1)}, f32[2,640,128]{1,2,0:T(8,128)S(1)}, u32[]{:S(2)}, u32[]{:S(2)}) %collective-permute-start.15) | collective-permute-done | bytes 655392 | tf_op jit(solution)/shard_map/ppermute | solution.py:19
  322.6 33.6 %all-reduce.21.cloned.1.call-done = f32[2,128,256]{1,2,0:T(8,128)} async-done(((f32[2,128,256]{1,2,0:T(8,128)}), f32[2,128,256]{1,2,0:T(8,128)}) %all-reduce.21.cloned.1.call-update) | async-done | bytes 262160 | tf_op jit(solution)/shard_map/psum | solution.py:158
  357.9 40.4 %all-reduce.5 = (f32[]{:T(128)}, f32[]{:T(128)}) all-reduce(f32[]{:T(128)} %get-tuple-element.16, f32[]{:T(128)} %get-tuple-element.15), channel_id=1, replica_groups=mesh['gx'=2,'gy'=4,'ma'=4] {'gx','gy','ma'}, use_global_device_ids=true, to_apply=%region_6.7 | all-reduce | flops 2 | bytes 16 | tf_op jit(solution)/shard_map/psum | solution.py:193
  417.4 10.6 %collective-permute-done.19 = f32[2,384,128]{1,2,0:T(8,128)S(1)} collective-permute-done((f32[2,384,128]{1,2,0:T(8,128)S(1)}, f32[2,384,128]{1,2,0:T(8,128)S(1)}, u32[]{:S(2)}, u32[]{:S(2)}) %collective-permute-start.19) | collective-permute-done | bytes 393248 | tf_op jit(solution)/shard_map/ppermute | solution.py:19
  435.4 36.2 %all-reduce.23.cloned.1.call-done = f32[2,256,256]{2,1,0:T(8,128)} async-done(((f32[2,256,256]{2,1,0:T(8,128)}), f32[2,256,256]{2,1,0:T(8,128)}) %all-reduce.23.cloned.1.call-update) | async-done | bytes 524304 | tf_op jit(solution)/shard_map/psum | solution.py:155
  489.3 8.2 %dynamic_update_slice.29 = f32[2,384,512]{1,2,0:T(8,128)S(1)} dynamic-update-slice(f32[2,384,512]{1,2,0:T(8,128)S(1)} %dynamic_update_slice.28, f32[2,256,256]{1,2,0:T(8,128)} %fusion.44, s32[]{:T(128)} %constant.15.clone.1, s32[]{:T(128)S(6)} %select_n.33, s32[]{:T(128)S(6)} %select_n.34) | dynamic-update-slice | bytes 1048580 | tf_op jit(solution)/shard_map/dynamic_update_slice | solution.py:166
  507.4 12.9 %collective-permute-done.22 = f32[2,640,128]{1,2,0:T(8,128)S(1)} collective-permute-done((f32[2,640,128]{1,2,0:T(8,128)S(1)}, f32[2,640,128]{1,2,0:T(8,128)S(1)}, u32[]{:S(2)}, u32[]{:S(2)}) %collective-permute-start.22) | collective-permute-done | bytes 655392 | tf_op jit(solution)/shard_map/ppermute | solution.py:16
  520.4 16.7 %collective-permute-done.23 = f32[2,640,128]{1,2,0:T(8,128)S(1)} collective-permute-done((f32[2,640,128]{1,2,0:T(8,128)S(1)}, f32[2,640,128]{1,2,0:T(8,128)S(1)}, u32[]{:S(2)}, u32[]{:S(2)}) %collective-permute-start.23) | collective-permute-done | bytes 655392 | tf_op jit(solution)/shard_map/ppermute | solution.py:19
  538.0 33.7 %all-reduce.25.cloned.1.call-done = f32[2,128,256]{1,2,0:T(8,128)} async-done(((f32[2,128,256]{1,2,0:T(8,128)}), f32[2,128,256]{1,2,0:T(8,128)}) %all-reduce.25.cloned.1.call-update) | async-done | bytes 262160 | tf_op jit(solution)/shard_map/psum | solution.py:158
  589.6 10.3 %collective-permute-done.27 = f32[2,384,128]{1,2,0:T(8,128)S(1)} collective-permute-done((f32[2,384,128]{1,2,0:T(8,128)S(1)}, f32[2,384,128]{1,2,0:T(8,128)S(1)}, u32[]{:S(2)}, u32[]{:S(2)}) %collective-permute-start.27) | collective-permute-done | bytes 393248 | tf_op jit(solution)/shard_map/ppermute | solution.py:19
  607.7 37.7 %all-reduce.27.cloned.1.call-done = f32[2,256,256]{2,1,0:T(8,128)} async-done(((f32[2,256,256]{2,1,0:T(8,128)}), f32[2,256,256]{2,1,0:T(8,128)}) %all-reduce.27.cloned.1.call-update) | async-done | bytes 524304 | tf_op jit(solution)/shard_map/psum | solution.py:155
  662.4 8.8 %dynamic_update_slice.31 = f32[2,384,512]{1,2,0:T(8,128)S(1)} dynamic-update-slice(f32[2,384,512]{1,2,0:T(8,128)S(1)} %dynamic_update_slice.30, f32[2,256,256]{1,2,0:T(8,128)S(1)} %fusion.41, s32[]{:T(128)} %constant.15.clone.1, s32[]{:T(128)S(6)} %select_n.33, s32[]{:T(128)S(6)} %select_n.34) | dynamic-update-slice | bytes 1048580 | tf_op jit(solution)/shard_map/dynamic_update_slice | solution.py:166
  681.1 12.9 %collective-permute-done.30 = f32[2,640,128]{1,2,0:T(8,128)S(1)} collective-permute-done((f32[2,640,128]{1,2,0:T(8,128)S(1)}, f32[2,640,128]{1,2,0:T(8,128)S(1)}, u32[]{:S(2)}, u32[]{:S(2)}) %collective-permute-start.30) | collective-permute-done | bytes 655392 | tf_op jit(solution)/shard_map/ppermute | solution.py:16
  694.1 16.9 %collective-permute-done.31 = f32[2,640,128]{1,2,0:T(8,128)S(1)} collective-permute-done((f32[2,640,128]{1,2,0:T(8,128)S(1)}, f32[2,640,128]{1,2,0:T(8,128)S(1)}, u32[]{:S(2)}, u32[]{:S(2)}) %collective-permute-start.31) | collective-permute-done | bytes 655392 | tf_op jit(solution)/shard_map/ppermute | solution.py:19
  712.0 33.7 %all-reduce.29.cloned.1.call-done = f32[2,128,256]{1,2,0:T(8,128)} async-done(((f32[2,128,256]{1,2,0:T(8,128)}), f32[2,128,256]{1,2,0:T(8,128)}) %all-reduce.29.cloned.1.call-update) | async-done | bytes 262160 | tf_op jit(solution)/shard_map/psum | solution.py:158
  747.6 40.4 %all-reduce.4 = (f32[]{:T(128)}, f32[]{:T(128)}) all-reduce(f32[]{:T(128)} %get-tuple-element.14, f32[]{:T(128)} %get-tuple-element.13), channel_id=1, replica_groups=mesh['gx'=2,'gy'=4,'ma'=4] {'gx','gy','ma'}, use_global_device_ids=true, to_apply=%region_20.21 | all-reduce | flops 2 | bytes 16 | tf_op jit(solution)/shard_map/psum | solution.py:193
  (272 shorter events, 232.4 us)
Async XLA Ops:
  6.5 75.1 %all-reduce.15.cloned.1.call-start = ((), (), s32[]{:S(2)}) async-start(), calls=%async_computation | async-start | bytes 1048576 | tf_op jit(solution)/shard_map/psum | solution.py:155
  13.7 17.3 %collective-permute-start.2 = (f32[2,384,128]{2,1,0:T(8,128)}, f32[2,384,128]{2,1,0:T(8,128)S(1)}, u32[]{:S(2)}, u32[]{:S(2)}) collective-permute-start(f32[2,384,128]{2,1,0:T(8,128)} %get-tuple-element.69), channel_id=1, source_target_pairs={{0,4},{4,8},{8,12},{1,5},{5,9},{9,13},{2,6},{6,10},{10,14},{3,7},{... | collective-permute-start | bytes 1179656 | tf_op jit(solution)/shard_map/ppermute | solution.py:16
  17.9 19.4 %collective-permute-start.3 = (f32[2,384,128]{2,1,0:T(8,128)}, f32[2,384,128]{2,1,0:T(8,128)}, u32[]{:S(2)}, u32[]{:S(2)}) collective-permute-start(f32[2,384,128]{2,1,0:T(8,128)} %get-tuple-element.70), channel_id=1, source_target_pairs={{4,0},{8,4},{12,8},{5,1},{9,5},{13,9},{6,2},{10,6},{14,10},{7,3},{... | collective-permute-start | bytes 1179656 | tf_op jit(solution)/shard_map/ppermute | solution.py:19
  42.5 139.8 %all-reduce.17.cloned.1.call-start = ((), (), s32[]{:S(2)}) async-start(), calls=%async_computation.1 | async-start | bytes 524288 | tf_op jit(solution)/shard_map/psum | solution.py:158
  112.8 17.5 %collective-permute-start.6 = (f32[2,640,128]{1,2,0:T(8,128)S(1)}, f32[2,640,128]{1,2,0:T(8,128)S(1)}, u32[]{:S(2)}, u32[]{:S(2)}) collective-permute-start(f32[2,640,128]{1,2,0:T(8,128)S(1)} %get-tuple-element.27), channel_id=1, source_target_pairs={{0,4},{4,8},{8,12},{1,5},{5,9},{9,13},{2,6},{6,10},{10,14},{3,7},{... | collective-permute-start | bytes 1966088 | tf_op jit(solution)/shard_map/ppermute | solution.py:16
  116.1 30.9 %collective-permute-start.7 = (f32[2,640,128]{1,2,0:T(8,128)S(1)}, f32[2,640,128]{1,2,0:T(8,128)S(1)}, u32[]{:S(2)}, u32[]{:S(2)}) collective-permute-start(f32[2,640,128]{1,2,0:T(8,128)S(1)} %get-tuple-element.28), channel_id=1, source_target_pairs={{4,0},{8,4},{12,8},{5,1},{9,5},{13,9},{6,2},{10,6},{14,10},{7,3},{... | collective-permute-start | bytes 1966088 | tf_op jit(solution)/shard_map/ppermute | solution.py:19
  148.5 107.5 %all-reduce.19.cloned.1.call-start = ((), (), s32[]{:S(2)}) async-start(), calls=%async_computation.2 | async-start | bytes 1048576 | tf_op jit(solution)/shard_map/psum | solution.py:155
  188.2 12.0 %collective-permute-start.10 = (f32[2,384,128]{1,2,0:T(8,128)S(1)}, f32[2,384,128]{1,2,0:T(8,128)S(1)}, u32[]{:S(2)}, u32[]{:S(2)}) collective-permute-start(f32[2,384,128]{1,2,0:T(8,128)S(1)} %get-tuple-element.67), channel_id=1, source_target_pairs={{0,4},{4,8},{8,12},{1,5},{5,9},{9,13},{2,6},{6,10},{10,14},{3,7},{... | collective-permute-start | bytes 1179656 | tf_op jit(solution)/shard_map/ppermute | solution.py:16
  191.6 19.0 %collective-permute-start.11 = (f32[2,384,128]{1,2,0:T(8,128)S(1)}, f32[2,384,128]{1,2,0:T(8,128)S(1)}, u32[]{:S(2)}, u32[]{:S(2)}) collective-permute-start(f32[2,384,128]{1,2,0:T(8,128)S(1)} %get-tuple-element.68), channel_id=1, source_target_pairs={{4,0},{8,4},{12,8},{5,1},{9,5},{13,9},{6,2},{10,6},{14,10},{7,3},{... | collective-permute-start | bytes 1179656 | tf_op jit(solution)/shard_map/ppermute | solution.py:19
  218.2 137.9 %all-reduce.21.cloned.1.call-start = ((), (), s32[]{:S(2)}) async-start(), calls=%async_computation.3 | async-start | bytes 524288 | tf_op jit(solution)/shard_map/psum | solution.py:158
  287.2 17.5 %collective-permute-start.14 = (f32[2,640,128]{1,2,0:T(8,128)S(1)}, f32[2,640,128]{1,2,0:T(8,128)S(1)}, u32[]{:S(2)}, u32[]{:S(2)}) collective-permute-start(f32[2,640,128]{1,2,0:T(8,128)S(1)} %get-tuple-element.25), channel_id=1, source_target_pairs={{0,4},{4,8},{8,12},{1,5},{5,9},{9,13},{2,6},{6,10},{10,14},{3,7},{... | collective-permute-start | bytes 1966088 | tf_op jit(solution)/shard_map/ppermute | solution.py:16
  290.5 30.9 %collective-permute-start.15 = (f32[2,640,128]{1,2,0:T(8,128)S(1)}, f32[2,640,128]{1,2,0:T(8,128)S(1)}, u32[]{:S(2)}, u32[]{:S(2)}) collective-permute-start(f32[2,640,128]{1,2,0:T(8,128)S(1)} %get-tuple-element.26), channel_id=1, source_target_pairs={{4,0},{8,4},{12,8},{5,1},{9,5},{13,9},{6,2},{10,6},{14,10},{7,3},{... | collective-permute-start | bytes 1966088 | tf_op jit(solution)/shard_map/ppermute | solution.py:19
  322.4 149.3 %all-reduce.23.cloned.1.call-start = ((), (), s32[]{:S(2)}) async-start(), calls=%async_computation.4 | async-start | bytes 1048576 | tf_op jit(solution)/shard_map/psum | solution.py:155
  404.6 12.8 %collective-permute-start.18 = (f32[2,384,128]{1,2,0:T(8,128)S(1)}, f32[2,384,128]{1,2,0:T(8,128)S(1)}, u32[]{:S(2)}, u32[]{:S(2)}) collective-permute-start(f32[2,384,128]{1,2,0:T(8,128)S(1)} %get-tuple-element.65), channel_id=1, source_target_pairs={{0,4},{4,8},{8,12},{1,5},{5,9},{9,13},{2,6},{6,10},{10,14},{3,7},{... | collective-permute-start | bytes 1179656 | tf_op jit(solution)/shard_map/ppermute | solution.py:16
  408.8 19.2 %collective-permute-start.19 = (f32[2,384,128]{1,2,0:T(8,128)S(1)}, f32[2,384,128]{1,2,0:T(8,128)S(1)}, u32[]{:S(2)}, u32[]{:S(2)}) collective-permute-start(f32[2,384,128]{1,2,0:T(8,128)S(1)} %get-tuple-element.66), channel_id=1, source_target_pairs={{4,0},{8,4},{12,8},{5,1},{9,5},{13,9},{6,2},{10,6},{14,10},{7,3},{... | collective-permute-start | bytes 1179656 | tf_op jit(solution)/shard_map/ppermute | solution.py:19
  435.1 136.6 %all-reduce.25.cloned.1.call-start = ((), (), s32[]{:S(2)}) async-start(), calls=%async_computation.5 | async-start | bytes 524288 | tf_op jit(solution)/shard_map/psum | solution.py:158
  502.8 17.5 %collective-permute-start.22 = (f32[2,640,128]{1,2,0:T(8,128)S(1)}, f32[2,640,128]{1,2,0:T(8,128)S(1)}, u32[]{:S(2)}, u32[]{:S(2)}) collective-permute-start(f32[2,640,128]{1,2,0:T(8,128)S(1)} %get-tuple-element.23), channel_id=1, source_target_pairs={{0,4},{4,8},{8,12},{1,5},{5,9},{9,13},{2,6},{6,10},{10,14},{3,7},{... | collective-permute-start | bytes 1966088 | tf_op jit(solution)/shard_map/ppermute | solution.py:16
  506.1 30.9 %collective-permute-start.23 = (f32[2,640,128]{1,2,0:T(8,128)S(1)}, f32[2,640,128]{1,2,0:T(8,128)S(1)}, u32[]{:S(2)}, u32[]{:S(2)}) collective-permute-start(f32[2,640,128]{1,2,0:T(8,128)S(1)} %get-tuple-element.24), channel_id=1, source_target_pairs={{4,0},{8,4},{12,8},{5,1},{9,5},{13,9},{6,2},{10,6},{14,10},{7,3},{... | collective-permute-start | bytes 1966088 | tf_op jit(solution)/shard_map/ppermute | solution.py:19
  538.0 107.5 %all-reduce.27.cloned.1.call-start = ((), (), s32[]{:S(2)}) async-start(), calls=%async_computation.6 | async-start | bytes 1048576 | tf_op jit(solution)/shard_map/psum | solution.py:155
  577.6 12.0 %collective-permute-start.26 = (f32[2,384,128]{1,2,0:T(8,128)S(1)}, f32[2,384,128]{1,2,0:T(8,128)S(1)}, u32[]{:S(2)}, u32[]{:S(2)}) collective-permute-start(f32[2,384,128]{1,2,0:T(8,128)S(1)} %get-tuple-element.63), channel_id=1, source_target_pairs={{0,4},{4,8},{8,12},{1,5},{5,9},{9,13},{2,6},{6,10},{10,14},{3,7},{... | collective-permute-start | bytes 1179656 | tf_op jit(solution)/shard_map/ppermute | solution.py:16
  581.0 19.0 %collective-permute-start.27 = (f32[2,384,128]{1,2,0:T(8,128)S(1)}, f32[2,384,128]{1,2,0:T(8,128)S(1)}, u32[]{:S(2)}, u32[]{:S(2)}) collective-permute-start(f32[2,384,128]{1,2,0:T(8,128)S(1)} %get-tuple-element.64), channel_id=1, source_target_pairs={{4,0},{8,4},{12,8},{5,1},{9,5},{13,9},{6,2},{10,6},{14,10},{7,3},{... | collective-permute-start | bytes 1179656 | tf_op jit(solution)/shard_map/ppermute | solution.py:19
  607.7 138.1 %all-reduce.29.cloned.1.call-start = ((), (), s32[]{:S(2)}) async-start(), calls=%async_computation.7 | async-start | bytes 524288 | tf_op jit(solution)/shard_map/psum | solution.py:158
  676.6 17.5 %collective-permute-start.30 = (f32[2,640,128]{1,2,0:T(8,128)S(1)}, f32[2,640,128]{1,2,0:T(8,128)S(1)}, u32[]{:S(2)}, u32[]{:S(2)}) collective-permute-start(f32[2,640,128]{1,2,0:T(8,128)S(1)} %get-tuple-element.21), channel_id=1, source_target_pairs={{0,4},{4,8},{8,12},{1,5},{5,9},{9,13},{2,6},{6,10},{10,14},{3,7},{... | collective-permute-start | bytes 1966088 | tf_op jit(solution)/shard_map/ppermute | solution.py:16
  679.8 31.2 %collective-permute-start.31 = (f32[2,640,128]{1,2,0:T(8,128)S(1)}, f32[2,640,128]{1,2,0:T(8,128)S(1)}, u32[]{:S(2)}, u32[]{:S(2)}) collective-permute-start(f32[2,640,128]{1,2,0:T(8,128)S(1)} %get-tuple-element.22), channel_id=1, source_target_pairs={{4,0},{8,4},{12,8},{5,1},{9,5},{13,9},{6,2},{10,6},{14,10},{7,3},{... | collective-permute-start | bytes 1966088 | tf_op jit(solution)/shard_map/ppermute | solution.py:19
  (49 other events, 458.3 us)
Sparse Core Ops, SparseCore 0:
  42.6 38.9 all-reduce.14
  148.7 33.5 all-reduce.16
  218.4 37.6 all-reduce.18
  322.5 33.5 all-reduce.20
  435.2 36.3 all-reduce.22
  538.1 33.5 all-reduce.24
  607.8 37.6 all-reduce.26
  712.1 33.5 all-reduce.28
where the time goes:
time: 808 us; the launch traced here: 797 us
  waiting for transfers between devices  478 us (59%)
  local copies, waits for them, and re-layouts  94.4 us (12%)
  blocking collectives  80.8 us (10%)
  starting transfers between devices  61.5 us (8%)
  other arithmetic  40.6 us (5%)
  between operations  26.1 us (3%)
  matrix products  15.7 us (2%)
    psum x4, waiting for transfers between devices, mode_total(): return lax.psum(partial_value, 'ma')  148 us
    psum x4, waiting for transfers between devices, combine(): summed = lax.psum(folded, 'ma')  135 us
    ppermute x16, waiting for transfers between devices, padded_2(): lax.ppermute(lax.slice_in_dim(block, 0, width, axis=dim), axis, backward)  121 us
    psum x2, blocking collectives, shards(): norm_now = lax.psum(local_sum(residual, residual), ('gx', 'gy', 'ma'))  80.8 us
    ppermute x16, waiting for transfers between devices, padded_2(): lax.ppermute(lax.slice_in_dim(block, block.shape[dim] - width, None, axis...  74.3 us
    dynamic_update_slice x8, local copies, waits for them, and re-layouts, project(): lax.dynamic_update_slice(extended, lax.dynamic_slice(extended, corner, (2...  65.2 us
    ppermute x16, starting transfers between devices, padded_2(): lax.ppermute(lax.slice_in_dim(block, block.shape[dim] - width, None, axis...  40.1 us
    ppermute x16, starting transfers between devices, padded_2(): lax.ppermute(lax.slice_in_dim(block, 0, width, axis=dim), axis, backward)  20.8 us
  transfers between devices with their start and end apart: 40, of which 35 were waited for; matrix products, arithmetic and copies ran while one was open for 1% of the time, Pallas kernels for 0%

commit v1 on v0

--- a/solution.py
+++ b/solution.py
@@ -190,7 +190,9 @@
         gradient = project(misfit, spectra)
         residual = -gradient
         direction = residual
-        norm_now = lax.psum(local_sum(residual, residual), ("gx", "gy", "ma"))
+        norm_now = jnp.sum(
+            lax.all_gather(local_sum(residual, residual), ("gx", "gy", "ma")), axis=0
+        )
         moved_spectra = spectra_of(direction)
         change = live_mask * mode_total(change_part(spectra, moved_spectra, mode_count))
         applied = project(change, spectra) + DAMPING * direction

time: 808 us -> 811 us (level)
    psum x2 -> x0, blocking collectives: 80.8 us -> none  [shards(): norm_now = lax.psum(local_sum(residual, residual), ('gx', 'gy', 'ma'))]
    unnamed x0 -> x2, blocking collectives: none -> 80.8 us
where the time goes in v1:
time: 811 us; the launch traced here: 800 us
  waiting for transfers between devices  479 us (59%)
  local copies, waits for them, and re-layouts  95.7 us (12%)
  blocking collectives  80.8 us (10%)
  starting transfers between devices  61.4 us (8%)
  other arithmetic  42 us (5%)
  between operations  25.8 us (3%)
  matrix products  15.7 us (2%)
    psum x4, waiting for transfers between devices, mode_total(): return lax.psum(partial_value, 'ma')  148 us
    psum x4, waiting for transfers between devices, combine(): summed = lax.psum(folded, 'ma')  135 us
    ppermute x16, waiting for transfers between devices, padded_2(): lax.ppermute(lax.slice_in_dim(block, 0, width, axis=dim), axis, backward)  121 us
    unnamed x2, blocking collectives  80.8 us
    ppermute x16, waiting for transfers between devices, padded_2(): lax.ppermute(lax.slice_in_dim(block, block.shape[dim] - width, None, axis...  74.3 us
    dynamic_update_slice x8, local copies, waits for them, and re-layouts, project(): lax.dynamic_update_slice(extended, lax.dynamic_slice(extended, corner, (2...  65.2 us
    ppermute x16, starting transfers between devices, padded_2(): lax.ppermute(lax.slice_in_dim(block, block.shape[dim] - width, None, axis...  40.1 us
    ppermute x16, starting transfers between devices, padded_2(): lax.ppermute(lax.slice_in_dim(block, 0, width, axis=dim), axis, backward)  20.8 us
  transfers between devices with their start and end apart: 40, of which 35 were waited for; matrix products, arithmetic and copies ran while one was open for 1% of the time, Pallas kernels for 0%

profile of v1, /device:TPU:0, one launch (start us, length us, event | category | flops | bytes accessed | tf_op | source)
XLA Modules:
  0.0 800.0 jit_solution(4215537090998334175)
XLA Ops:
  45.2 36.4 %all-reduce.17.cloned.1.call-done = f32[2,256,256]{2,1,0:T(8,128)} async-done(((f32[2,256,256]{2,1,0:T(8,128)}), f32[2,256,256]{2,1,0:T(8,128)}) %all-reduce.17.cloned.1.call-update) | async-done | bytes 524304 | tf_op jit(solution)/shard_map/psum | solution.py:155
  99.3 8.2 %dynamic_update_slice.25 = f32[2,384,512]{1,2,0:T(8,128)S(1)} dynamic-update-slice(f32[2,384,512]{1,2,0:T(8,128)S(1)} %dynamic_update_slice.24, f32[2,256,256]{1,2,0:T(8,128)} %fusion.50, s32[]{:T(128)} %constant.15.clone.1, s32[]{:T(128)S(6)} %select_n.33, s32[]{:T(128)S(6)} %select_n.34) | dynamic-update-slice | bytes 1048580 | tf_op jit(solution)/shard_map/dynamic_update_slice | solution.py:166
  117.5 12.9 %collective-permute-done.6 = f32[2,640,128]{1,2,0:T(8,128)S(1)} collective-permute-done((f32[2,640,128]{1,2,0:T(8,128)S(1)}, f32[2,640,128]{1,2,0:T(8,128)S(1)}, u32[]{:S(2)}, u32[]{:S(2)}) %collective-permute-start.6) | collective-permute-done | bytes 655392 | tf_op jit(solution)/shard_map/ppermute | solution.py:16
  130.4 16.7 %collective-permute-done.7 = f32[2,640,128]{1,2,0:T(8,128)S(1)} collective-permute-done((f32[2,640,128]{1,2,0:T(8,128)S(1)}, f32[2,640,128]{1,2,0:T(8,128)S(1)}, u32[]{:S(2)}, u32[]{:S(2)}) %collective-permute-start.7) | collective-permute-done | bytes 655392 | tf_op jit(solution)/shard_map/ppermute | solution.py:19
  148.7 33.7 %all-reduce.19.cloned.1.call-done = f32[2,128,256]{1,2,0:T(8,128)} async-done(((f32[2,128,256]{1,2,0:T(8,128)}), f32[2,128,256]{1,2,0:T(8,128)}) %all-reduce.19.cloned.1.call-update) | async-done | bytes 262160 | tf_op jit(solution)/shard_map/psum | solution.py:158
  200.2 10.3 %collective-permute-done.11 = f32[2,384,128]{1,2,0:T(8,128)S(1)} collective-permute-done((f32[2,384,128]{1,2,0:T(8,128)S(1)}, f32[2,384,128]{1,2,0:T(8,128)S(1)}, u32[]{:S(2)}, u32[]{:S(2)}) %collective-permute-start.11) | collective-permute-done | bytes 393248 | tf_op jit(solution)/shard_map/ppermute | solution.py:19
  218.3 37.7 %all-reduce.21.cloned.1.call-done = f32[2,256,256]{2,1,0:T(8,128)} async-done(((f32[2,256,256]{2,1,0:T(8,128)}), f32[2,256,256]{2,1,0:T(8,128)}) %all-reduce.21.cloned.1.call-update) | async-done | bytes 524304 | tf_op jit(solution)/shard_map/psum | solution.py:155
  273.7 8.2 %dynamic_update_slice.27 = f32[2,384,512]{1,2,0:T(8,128)S(1)} dynamic-update-slice(f32[2,384,512]{1,2,0:T(8,128)S(1)} %dynamic_update_slice.26, f32[2,256,256]{1,2,0:T(8,128)} %fusion.47, s32[]{:T(128)} %constant.15.clone.1, s32[]{:T(128)S(6)} %select_n.33, s32[]{:T(128)S(6)} %select_n.34) | dynamic-update-slice | bytes 1048580 | tf_op jit(solution)/shard_map/dynamic_update_slice | solution.py:166
  291.8 12.9 %collective-permute-done.14 = f32[2,640,128]{1,2,0:T(8,128)S(1)} collective-permute-done((f32[2,640,128]{1,2,0:T(8,128)S(1)}, f32[2,640,128]{1,2,0:T(8,128)S(1)}, u32[]{:S(2)}, u32[]{:S(2)}) %collective-permute-start.14) | collective-permute-done | bytes 655392 | tf_op jit(solution)/shard_map/ppermute | solution.py:16
  304.7 16.7 %collective-permute-done.15 = f32[2,640,128]{1,2,0:T(8,128)S(1)} collective-permute-done((f32[2,640,128]{1,2,0:T(8,128)S(1)}, f32[2,640,128]{1,2,0:T(8,128)S(1)}, u32[]{:S(2)}, u32[]{:S(2)}) %collective-permute-start.15) | collective-permute-done | bytes 655392 | tf_op jit(solution)/shard_map/ppermute | solution.py:19
  322.6 33.5 %all-reduce.23.cloned.1.call-done = f32[2,128,256]{1,2,0:T(8,128)} async-done(((f32[2,128,256]{1,2,0:T(8,128)}), f32[2,128,256]{1,2,0:T(8,128)}) %all-reduce.23.cloned.1.call-update) | async-done | bytes 262160 | tf_op jit(solution)/shard_map/psum | solution.py:158
  358.7 40.4 %all-reduce.7 = (f32[32]{0:T(128)S(1)}, f32[]{:T(128)}) all-reduce(f32[32]{0:T(128)S(1)} %dynamic-update-slice, f32[]{:T(128)} %get-tuple-element.15), channel_id=1, replica_groups=mesh['gx'=2,'gy'=4,'ma'=4] {'gx','gy','ma'}, use_global_device_ids=true, to_apply=%add.4 | all-reduce | flops 33 | bytes 264
  418.8 10.5 %collective-permute-done.19 = f32[2,384,128]{1,2,0:T(8,128)S(1)} collective-permute-done((f32[2,384,128]{1,2,0:T(8,128)S(1)}, f32[2,384,128]{1,2,0:T(8,128)S(1)}, u32[]{:S(2)}, u32[]{:S(2)}) %collective-permute-start.19) | collective-permute-done | bytes 393248 | tf_op jit(solution)/shard_map/ppermute | solution.py:19
  436.7 36.2 %all-reduce.25.cloned.1.call-done = f32[2,256,256]{2,1,0:T(8,128)} async-done(((f32[2,256,256]{2,1,0:T(8,128)}), f32[2,256,256]{2,1,0:T(8,128)}) %all-reduce.25.cloned.1.call-update) | async-done | bytes 524304 | tf_op jit(solution)/shard_map/psum | solution.py:155
  508.8 12.9 %collective-permute-done.22 = f32[2,640,128]{1,2,0:T(8,128)S(1)} collective-permute-done((f32[2,640,128]{1,2,0:T(8,128)S(1)}, f32[2,640,128]{1,2,0:T(8,128)S(1)}, u32[]{:S(2)}, u32[]{:S(2)}) %collective-permute-start.22) | collective-permute-done | bytes 655392 | tf_op jit(solution)/shard_map/ppermute | solution.py:16
  521.8 16.7 %collective-permute-done.23 = f32[2,640,128]{1,2,0:T(8,128)S(1)} collective-permute-done((f32[2,640,128]{1,2,0:T(8,128)S(1)}, f32[2,640,128]{1,2,0:T(8,128)S(1)}, u32[]{:S(2)}, u32[]{:S(2)}) %collective-permute-start.23) | collective-permute-done | bytes 655392 | tf_op jit(solution)/shard_map/ppermute | solution.py:19
  539.5 33.7 %all-reduce.27.cloned.1.call-done = f32[2,128,256]{1,2,0:T(8,128)} async-done(((f32[2,128,256]{1,2,0:T(8,128)}), f32[2,128,256]{1,2,0:T(8,128)}) %all-reduce.27.cloned.1.call-update) | async-done | bytes 262160 | tf_op jit(solution)/shard_map/psum | solution.py:158
  591.1 10.3 %collective-permute-done.27 = f32[2,384,128]{1,2,0:T(8,128)S(1)} collective-permute-done((f32[2,384,128]{1,2,0:T(8,128)S(1)}, f32[2,384,128]{1,2,0:T(8,128)S(1)}, u32[]{:S(2)}, u32[]{:S(2)}) %collective-permute-start.27) | collective-permute-done | bytes 393248 | tf_op jit(solution)/shard_map/ppermute | solution.py:19
  609.1 37.7 %all-reduce.29.cloned.1.call-done = f32[2,256,256]{2,1,0:T(8,128)} async-done(((f32[2,256,256]{2,1,0:T(8,128)}), f32[2,256,256]{2,1,0:T(8,128)}) %all-reduce.29.cloned.1.call-update) | async-done | bytes 524304 | tf_op jit(solution)/shard_map/psum | solution.py:155
  663.8 8.8 %dynamic_update_slice.31 = f32[2,384,512]{1,2,0:T(8,128)S(1)} dynamic-update-slice(f32[2,384,512]{1,2,0:T(8,128)S(1)} %dynamic_update_slice.30, f32[2,256,256]{1,2,0:T(8,128)S(1)} %fusion.41, s32[]{:T(128)} %constant.15.clone.1, s32[]{:T(128)S(6)} %select_n.33, s32[]{:T(128)S(6)} %select_n.34) | dynamic-update-slice | bytes 1048580 | tf_op jit(solution)/shard_map/dynamic_update_slice | solution.py:166
  682.5 12.9 %collective-permute-done.30 = f32[2,640,128]{1,2,0:T(8,128)S(1)} collective-permute-done((f32[2,640,128]{1,2,0:T(8,128)S(1)}, f32[2,640,128]{1,2,0:T(8,128)S(1)}, u32[]{:S(2)}, u32[]{:S(2)}) %collective-permute-start.30) | collective-permute-done | bytes 655392 | tf_op jit(solution)/shard_map/ppermute | solution.py:16
  695.4 16.9 %collective-permute-done.31 = f32[2,640,128]{1,2,0:T(8,128)S(1)} collective-permute-done((f32[2,640,128]{1,2,0:T(8,128)S(1)}, f32[2,640,128]{1,2,0:T(8,128)S(1)}, u32[]{:S(2)}, u32[]{:S(2)}) %collective-permute-start.31) | collective-permute-done | bytes 655392 | tf_op jit(solution)/shard_map/ppermute | solution.py:19
  713.4 33.8 %all-reduce.31.cloned.1.call-done = f32[2,128,256]{1,2,0:T(8,128)} async-done(((f32[2,128,256]{1,2,0:T(8,128)}), f32[2,128,256]{1,2,0:T(8,128)}) %all-reduce.31.cloned.1.call-update) | async-done | bytes 262160 | tf_op jit(solution)/shard_map/psum | solution.py:158
  749.6 40.4 %all-reduce.6 = (f32[32]{0:T(128)S(1)}, f32[]{:T(128)}) all-reduce(f32[32]{0:T(128)S(1)} %dynamic-update-slice.1, f32[]{:T(128)} %get-tuple-element.13), channel_id=1, replica_groups=mesh['gx'=2,'gy'=4,'ma'=4] {'gx','gy','ma'}, use_global_device_ids=true, to_apply=%add.5 | all-reduce | flops 33 | bytes 264
  (278 shorter events, 235.5 us)
Async XLA Ops:
  6.5 75.0 %all-reduce.17.cloned.1.call-start = ((), (), s32[]{:S(2)}) async-start(), calls=%async_computation | async-start | bytes 1048576 | tf_op jit(solution)/shard_map/psum | solution.py:155
  13.7 17.1 %collective-permute-start.2 = (f32[2,384,128]{2,1,0:T(8,128)}, f32[2,384,128]{2,1,0:T(8,128)S(1)}, u32[]{:S(2)}, u32[]{:S(2)}) collective-permute-start(f32[2,384,128]{2,1,0:T(8,128)} %get-tuple-element.69), channel_id=1, source_target_pairs={{0,4},{4,8},{8,12},{1,5},{5,9},{9,13},{2,6},{6,10},{10,14},{3,7},{... | collective-permute-start | bytes 1179656 | tf_op jit(solution)/shard_map/ppermute | solution.py:16
  17.9 19.4 %collective-permute-start.3 = (f32[2,384,128]{2,1,0:T(8,128)}, f32[2,384,128]{2,1,0:T(8,128)}, u32[]{:S(2)}, u32[]{:S(2)}) collective-permute-start(f32[2,384,128]{2,1,0:T(8,128)} %get-tuple-element.70), channel_id=1, source_target_pairs={{4,0},{8,4},{12,8},{5,1},{9,5},{13,9},{6,2},{10,6},{14,10},{7,3},{... | collective-permute-start | bytes 1179656 | tf_op jit(solution)/shard_map/ppermute | solution.py:19
  42.5 139.8 %all-reduce.19.cloned.1.call-start = ((), (), s32[]{:S(2)}) async-start(), calls=%async_computation.1 | async-start | bytes 524288 | tf_op jit(solution)/shard_map/psum | solution.py:158
  112.9 17.5 %collective-permute-start.6 = (f32[2,640,128]{1,2,0:T(8,128)S(1)}, f32[2,640,128]{1,2,0:T(8,128)S(1)}, u32[]{:S(2)}, u32[]{:S(2)}) collective-permute-start(f32[2,640,128]{1,2,0:T(8,128)S(1)} %get-tuple-element.27), channel_id=1, source_target_pairs={{0,4},{4,8},{8,12},{1,5},{5,9},{9,13},{2,6},{6,10},{10,14},{3,7},{... | collective-permute-start | bytes 1966088 | tf_op jit(solution)/shard_map/ppermute | solution.py:16
  116.2 30.9 %collective-permute-start.7 = (f32[2,640,128]{1,2,0:T(8,128)S(1)}, f32[2,640,128]{1,2,0:T(8,128)S(1)}, u32[]{:S(2)}, u32[]{:S(2)}) collective-permute-start(f32[2,640,128]{1,2,0:T(8,128)S(1)} %get-tuple-element.28), channel_id=1, source_target_pairs={{4,0},{8,4},{12,8},{5,1},{9,5},{13,9},{6,2},{10,6},{14,10},{7,3},{... | collective-permute-start | bytes 1966088 | tf_op jit(solution)/shard_map/ppermute | solution.py:19
  148.6 107.5 %all-reduce.21.cloned.1.call-start = ((), (), s32[]{:S(2)}) async-start(), calls=%async_computation.2 | async-start | bytes 1048576 | tf_op jit(solution)/shard_map/psum | solution.py:155
  188.2 12.0 %collective-permute-start.10 = (f32[2,384,128]{1,2,0:T(8,128)S(1)}, f32[2,384,128]{1,2,0:T(8,128)S(1)}, u32[]{:S(2)}, u32[]{:S(2)}) collective-permute-start(f32[2,384,128]{1,2,0:T(8,128)S(1)} %get-tuple-element.67), channel_id=1, source_target_pairs={{0,4},{4,8},{8,12},{1,5},{5,9},{9,13},{2,6},{6,10},{10,14},{3,7},{... | collective-permute-start | bytes 1179656 | tf_op jit(solution)/shard_map/ppermute | solution.py:16
  191.6 19.0 %collective-permute-start.11 = (f32[2,384,128]{1,2,0:T(8,128)S(1)}, f32[2,384,128]{1,2,0:T(8,128)S(1)}, u32[]{:S(2)}, u32[]{:S(2)}) collective-permute-start(f32[2,384,128]{1,2,0:T(8,128)S(1)} %get-tuple-element.68), channel_id=1, source_target_pairs={{4,0},{8,4},{12,8},{5,1},{9,5},{13,9},{6,2},{10,6},{14,10},{7,3},{... | collective-permute-start | bytes 1179656 | tf_op jit(solution)/shard_map/ppermute | solution.py:19
  218.3 137.9 %all-reduce.23.cloned.1.call-start = ((), (), s32[]{:S(2)}) async-start(), calls=%async_computation.3 | async-start | bytes 524288 | tf_op jit(solution)/shard_map/psum | solution.py:158
  287.2 17.5 %collective-permute-start.14 = (f32[2,640,128]{1,2,0:T(8,128)S(1)}, f32[2,640,128]{1,2,0:T(8,128)S(1)}, u32[]{:S(2)}, u32[]{:S(2)}) collective-permute-start(f32[2,640,128]{1,2,0:T(8,128)S(1)} %get-tuple-element.25), channel_id=1, source_target_pairs={{0,4},{4,8},{8,12},{1,5},{5,9},{9,13},{2,6},{6,10},{10,14},{3,7},{... | collective-permute-start | bytes 1966088 | tf_op jit(solution)/shard_map/ppermute | solution.py:16
  290.5 30.9 %collective-permute-start.15 = (f32[2,640,128]{1,2,0:T(8,128)S(1)}, f32[2,640,128]{1,2,0:T(8,128)S(1)}, u32[]{:S(2)}, u32[]{:S(2)}) collective-permute-start(f32[2,640,128]{1,2,0:T(8,128)S(1)} %get-tuple-element.26), channel_id=1, source_target_pairs={{4,0},{8,4},{12,8},{5,1},{9,5},{13,9},{6,2},{10,6},{14,10},{7,3},{... | collective-permute-start | bytes 1966088 | tf_op jit(solution)/shard_map/ppermute | solution.py:19
  322.4 150.5 %all-reduce.25.cloned.1.call-start = ((), (), s32[]{:S(2)}) async-start(), calls=%async_computation.4 | async-start | bytes 1048576 | tf_op jit(solution)/shard_map/psum | solution.py:155
  405.9 12.8 %collective-permute-start.18 = (f32[2,384,128]{1,2,0:T(8,128)S(1)}, f32[2,384,128]{1,2,0:T(8,128)S(1)}, u32[]{:S(2)}, u32[]{:S(2)}) collective-permute-start(f32[2,384,128]{1,2,0:T(8,128)S(1)} %get-tuple-element.65), channel_id=1, source_target_pairs={{0,4},{4,8},{8,12},{1,5},{5,9},{9,13},{2,6},{6,10},{10,14},{3,7},{... | collective-permute-start | bytes 1179656 | tf_op jit(solution)/shard_map/ppermute | solution.py:16
  410.2 19.2 %collective-permute-start.19 = (f32[2,384,128]{1,2,0:T(8,128)S(1)}, f32[2,384,128]{1,2,0:T(8,128)S(1)}, u32[]{:S(2)}, u32[]{:S(2)}) collective-permute-start(f32[2,384,128]{1,2,0:T(8,128)S(1)} %get-tuple-element.66), channel_id=1, source_target_pairs={{4,0},{8,4},{12,8},{5,1},{9,5},{13,9},{6,2},{10,6},{14,10},{7,3},{... | collective-permute-start | bytes 1179656 | tf_op jit(solution)/shard_map/ppermute | solution.py:19
  436.4 136.8 %all-reduce.27.cloned.1.call-start = ((), (), s32[]{:S(2)}) async-start(), calls=%async_computation.5 | async-start | bytes 524288 | tf_op jit(solution)/shard_map/psum | solution.py:158
  504.2 17.5 %collective-permute-start.22 = (f32[2,640,128]{1,2,0:T(8,128)S(1)}, f32[2,640,128]{1,2,0:T(8,128)S(1)}, u32[]{:S(2)}, u32[]{:S(2)}) collective-permute-start(f32[2,640,128]{1,2,0:T(8,128)S(1)} %get-tuple-element.23), channel_id=1, source_target_pairs={{0,4},{4,8},{8,12},{1,5},{5,9},{9,13},{2,6},{6,10},{10,14},{3,7},{... | collective-permute-start | bytes 1966088 | tf_op jit(solution)/shard_map/ppermute | solution.py:16
  507.5 30.9 %collective-permute-start.23 = (f32[2,640,128]{1,2,0:T(8,128)S(1)}, f32[2,640,128]{1,2,0:T(8,128)S(1)}, u32[]{:S(2)}, u32[]{:S(2)}) collective-permute-start(f32[2,640,128]{1,2,0:T(8,128)S(1)} %get-tuple-element.24), channel_id=1, source_target_pairs={{4,0},{8,4},{12,8},{5,1},{9,5},{13,9},{6,2},{10,6},{14,10},{7,3},{... | collective-permute-start | bytes 1966088 | tf_op jit(solution)/shard_map/ppermute | solution.py:19
  539.4 107.4 %all-reduce.29.cloned.1.call-start = ((), (), s32[]{:S(2)}) async-start(), calls=%async_computation.6 | async-start | bytes 1048576 | tf_op jit(solution)/shard_map/psum | solution.py:155
  579.0 12.0 %collective-permute-start.26 = (f32[2,384,128]{1,2,0:T(8,128)S(1)}, f32[2,384,128]{1,2,0:T(8,128)S(1)}, u32[]{:S(2)}, u32[]{:S(2)}) collective-permute-start(f32[2,384,128]{1,2,0:T(8,128)S(1)} %get-tuple-element.63), channel_id=1, source_target_pairs={{0,4},{4,8},{8,12},{1,5},{5,9},{9,13},{2,6},{6,10},{10,14},{3,7},{... | collective-permute-start | bytes 1179656 | tf_op jit(solution)/shard_map/ppermute | solution.py:16
  582.4 19.0 %collective-permute-start.27 = (f32[2,384,128]{1,2,0:T(8,128)S(1)}, f32[2,384,128]{1,2,0:T(8,128)S(1)}, u32[]{:S(2)}, u32[]{:S(2)}) collective-permute-start(f32[2,384,128]{1,2,0:T(8,128)S(1)} %get-tuple-element.64), channel_id=1, source_target_pairs={{4,0},{8,4},{12,8},{5,1},{9,5},{13,9},{6,2},{10,6},{14,10},{7,3},{... | collective-permute-start | bytes 1179656 | tf_op jit(solution)/shard_map/ppermute | solution.py:19
  609.1 138.0 %all-reduce.31.cloned.1.call-start = ((), (), s32[]{:S(2)}) async-start(), calls=%async_computation.7 | async-start | bytes 524288 | tf_op jit(solution)/shard_map/psum | solution.py:158
  678.0 17.5 %collective-permute-start.30 = (f32[2,640,128]{1,2,0:T(8,128)S(1)}, f32[2,640,128]{1,2,0:T(8,128)S(1)}, u32[]{:S(2)}, u32[]{:S(2)}) collective-permute-start(f32[2,640,128]{1,2,0:T(8,128)S(1)} %get-tuple-element.21), channel_id=1, source_target_pairs={{0,4},{4,8},{8,12},{1,5},{5,9},{9,13},{2,6},{6,10},{10,14},{3,7},{... | collective-permute-start | bytes 1966088 | tf_op jit(solution)/shard_map/ppermute | solution.py:16
  681.2 31.1 %collective-permute-start.31 = (f32[2,640,128]{1,2,0:T(8,128)S(1)}, f32[2,640,128]{1,2,0:T(8,128)S(1)}, u32[]{:S(2)}, u32[]{:S(2)}) collective-permute-start(f32[2,640,128]{1,2,0:T(8,128)S(1)} %get-tuple-element.22), channel_id=1, source_target_pairs={{4,0},{8,4},{12,8},{5,1},{9,5},{13,9},{6,2},{10,6},{14,10},{7,3},{... | collective-permute-start | bytes 1966088 | tf_op jit(solution)/shard_map/ppermute | solution.py:19
  (49 other events, 462.5 us)
Sparse Core Ops, SparseCore 0:
  42.6 38.8 all-reduce.16
  148.7 33.5 all-reduce.18
  218.4 37.6 all-reduce.20
  322.5 33.5 all-reduce.22
  436.6 36.3 all-reduce.24
  539.6 33.5 all-reduce.26
  609.2 37.6 all-reduce.28
  713.5 33.5 all-reduce.30
